TPU v7x, 512 devices: a 4x2x32 block of a 4x8x32 slice. The times are simulated.
512 devices in a mesh: groups: 2 (over y), blk: 64 (over z, core), head: 4 (over x).
Axes of the slice: x: 4, y: 2, z: 32, core: 2. Of those that a mesh axis runs over, the one named last changes fastest.
The devices are a block of a 4x8x32 slice.
Arguments:
- queries: bfloat16 [4, 64, 8192], P('groups', 'blk', 'head'), parts along dimension 0, may hold values from -4.5 to 4.5
- stored_cache_keys: bfloat16 [4, 32768, 1024], P('groups', 'blk', 'head'), parts along dimension 0, may hold values from -4.5 to 4.5
- stored_cache_values: bfloat16 [4, 32768, 1024], P('groups', 'blk', 'head'), parts along dimension 0, may hold values from -6 to 6
- out_weight: bfloat16 [8192, 8192], P('head', 'blk'), may hold values from -3 to 3
- lengths: int32 [4], P('groups'), parts along dimension 0, may hold values from 16384 to 32768
Outputs:
- projected: bfloat16 [4, 64, 8192], P('groups', 'head', 'blk'), parts along dimension 0
There are 2 independent parts, one for each index of `groups`. A program takes and returns all parts, laid end to end along the dimension named above; an argument that names none is the same for every part. Nothing has to cross between parts.
All inputs are finite; a program needn't handle non-finite values.
Results may differ from a plain program's by a relative error of at most 0.0056.
Values may be sent and summed in bfloat16 or wider, within the bound.
No kernel may reach another device: no remote copies, remote signals or barrier semaphores. Data moves between devices by JAX's collectives and lax.ppermute only.
A program may use at most 64 MiB of HBM per device.

v0:
```python
import math
import jax
import jax.numpy as jnp
from jax import lax
from jax.sharding import Mesh
from jax.sharding import PartitionSpec as P

REQUEST_COUNT = 2
QUERY_HEAD_COUNT = 64
KEY_VALUE_HEADS = 8
HEAD_DIMENSION = 128
BLK = ("blk_0", "blk_1")
masked_fill_value = -1e30


def in_one_piece(arrays, axis, split_dim, concat_dim, along):
    ends, at = ([], 0)
    for a in arrays[:-1]:
        at += a.shape[along]
        ends.append(at)
    both = jnp.concatenate(arrays, axis=along)
    return tuple(
        jnp.split(
            lax.all_to_all(both, axis, split_axis=split_dim, concat_axis=concat_dim, tiled=True),
            ends,
            axis=along,
        )
    )


def joined_along(pieces, dim):
    shape = list(pieces.shape[1:])
    shape[dim] *= pieces.shape[0]
    return jnp.moveaxis(pieces, 0, dim).reshape(shape)


def gather_in_order(value, axes, order):
    pieces = value
    for k in order:
        pieces = lax.all_gather(pieces, axes[k])
    done = order[::-1]
    back = [done.index(k) for k in range(len(axes))]
    pieces = pieces.transpose(*back, *range(len(axes), pieces.ndim))
    return pieces.reshape(-1, *value.shape)


def gathered_by_axis(value, axes, order, dim):
    return joined_along(gather_in_order(value, axes, order), dim)


def in_blocks(value, dim, peers):
    before, after = (value.shape[:dim], value.shape[dim + 1 :])
    return jnp.moveaxis(value.reshape(*before, peers, -1, *after), dim, 0)


def sent_and_summed(value, axis, dim):
    pieces = in_blocks(value, dim, lax.axis_size(axis))
    arrived = lax.all_to_all(pieces, axis, split_axis=0, concat_axis=0, tiled=True)
    return arrived.sum(axis=0)


def body(queries, stored_cache_keys, stored_cache_values, out_weight, lengths):
    group_width = QUERY_HEAD_COUNT // KEY_VALUE_HEADS
    local_heads = stored_cache_keys.shape[2] // HEAD_DIMENSION
    query_heads = local_heads * group_width
    span = stored_cache_keys.shape[1]
    new_count = queries.shape[1] * lax.axis_size(BLK)
    key_pos = lax.axis_index(BLK) * span + jnp.arange(span, dtype=jnp.int32)
    score_scale = 1.0 / math.sqrt(HEAD_DIMENSION)
    piece = lax.all_gather(queries, BLK, axis=1, tiled=True)
    rows_count = piece.shape[1]
    query_pos = lengths[:, None] - new_count + jnp.arange(rows_count, dtype=jnp.int32)[None, :]
    sums_list = []
    maxima_list = []
    totals_list = []
    for request in range(REQUEST_COUNT):
        visible = (key_pos[None, :] <= query_pos[request][:, None])[:, None, :]
        parts_sum, parts_max, parts_total = ([], [], [])
        for kv_head in range(local_heads):
            block_query = piece[
                request,
                :,
                kv_head
                * group_width
                * HEAD_DIMENSION : (kv_head + 1)
                * group_width
                * HEAD_DIMENSION,
            ].reshape(rows_count, group_width, HEAD_DIMENSION)
            local_keys = stored_cache_keys[
                request, :, kv_head * HEAD_DIMENSION : (kv_head + 1) * HEAD_DIMENSION
            ]
            local_values = stored_cache_values[
                request, :, kv_head * HEAD_DIMENSION : (kv_head + 1) * HEAD_DIMENSION
            ]
            scores = (
                jnp.einsum(
                    "ngd,cd->ngc", block_query, local_keys, preferred_element_type=jnp.float32
                )
                * score_scale
            )
            block_max = jnp.max(jnp.where(visible, scores, masked_fill_value), axis=-1)
            weights = jnp.where(visible, jnp.exp(scores - block_max[..., None]), 0.0)
            parts_total.append(jnp.sum(weights, axis=-1))
            parts_max.append(block_max)
            weighted = jnp.einsum(
                "ngc,cd->ngd",
                weights.astype(jnp.bfloat16),
                local_values,
                preferred_element_type=jnp.float32,
            )
            parts_sum.append(weighted.reshape(rows_count, group_width * HEAD_DIMENSION))
        sums_list.append(jnp.concatenate(parts_sum, axis=1))
        maxima_list.append(jnp.concatenate(parts_max, axis=1))
        totals_list.append(jnp.concatenate(parts_total, axis=1))
    new_sums = jnp.stack(sums_list, axis=0)
    new_maxima = jnp.stack(maxima_list, axis=0)
    new_totals = jnp.stack(totals_list, axis=0)
    received = in_one_piece((new_sums[None], new_maxima[None], new_totals[None]), BLK, 2, 0, 3)
    part_sums, part_max, part_totals = received
    blocks = part_sums.shape[0]
    own_rows = part_sums.shape[2]
    top = jnp.max(part_max, axis=0)
    factor = jnp.exp(part_max - top[None])
    overall = jnp.sum(factor * part_totals, axis=0)
    shaped = part_sums.reshape(blocks, REQUEST_COUNT, own_rows, query_heads, HEAD_DIMENSION)
    merged = jnp.sum(shaped * factor[..., None], axis=0) / overall[..., None]
    own_attention = merged.astype(jnp.bfloat16).reshape(
        REQUEST_COUNT, own_rows, query_heads * HEAD_DIMENSION
    )
    terms = jnp.einsum(
        "rnc,cd->rnd",
        gathered_by_axis(own_attention, BLK, (0, 1), 1),
        out_weight,
        preferred_element_type=jnp.float32,
    )
    return sent_and_summed(terms, "head", 1).astype(jnp.bfloat16)


def solution(mesh):
    torus = Mesh(
        mesh.devices.reshape(mesh.shape["groups"], 32, 2, mesh.shape["head"]),
        ("groups", "blk_0", "blk_1", "head"),
    )
    return jax.shard_map(
        body,
        mesh=torus,
        in_specs=(
            P("groups", BLK, "head"),
            P("groups", BLK, "head"),
            P("groups", BLK, "head"),
            P("head", BLK),
            P("groups"),
        ),
        out_specs=P("groups", "head", BLK),
        check_vma=False,
    )
```

profile of v0, /device:TPU:40, one launch (start us, length us, event | category | flops | bytes accessed | tf_op | source)
XLA Modules:
  0.0 312.7 jit_solution(946098355099298313)
XLA Ops:
  0.0 0.0 copy-start
  0.0 0.7 broadcast_add_fusion
  0.7 0.1 iota_add_fusion.1
  0.8 97.1 %all_gather.12 = bf16[2,64,2048]{2,0,1:T(2,128)(2,1)S(1)} all-gather(bf16[2,1,2048]{2,0,1:T(2,128)(2,1)} %param.5), channel_id=1, replica_groups=mesh['groups'=2,'blk_0'=32,'blk_1'=2,'head'=4] {'blk_0','blk_1'}, dimensions={1}, use_global_device_ids=true | all-gather | bytes 532480 | tf_op jit(solution)/shard_map/all_gather | solution.py:70
  97.9 2.3 slice_reduce_fusion.3
  100.3 0.7 copy.35
  100.9 0.1 broadcast_compare_fusion.1
  101.0 1.3 select_reduce_fusion.1
  102.4 0.1 copy.20
  102.5 1.3 fusion.11
  103.7 2.1 fusion.5
  105.9 0.1 copy.21
  105.9 1.3 fusion.9
  107.2 1.3 select_reduce_fusion.3
  108.6 0.1 copy.18
  108.7 1.4 fusion.15
  110.1 2.6 fusion.1
  112.7 0.1 copy.19
  112.8 1.3 fusion.3
  114.1 1.3 fusion.13
  115.4 0.1 copy.25
  115.5 0.1 copy_bitcast_fusion
  115.7 0.4 stack.28
  116.0 0.3 copy-done.6
  116.4 0.1 copy.23
  116.4 0.1 copy.24
  116.5 0.1 copy.26
  116.6 0.1 copy_bitcast_fusion.2
  116.7 0.4 stack.27
  117.1 0.1 copy.22
  117.2 0.1 copy.27
  117.3 0.9 maximum_bitcast_fusion
  118.3 2.1 concatenate.27
  120.4 121.5 %all_to_all.23 = f32[1,2,64,2080]{3,1,0,2:T(2,128)S(1)} all-to-all(f32[1,2,64,2080]{3,1,0,2:T(2,128)S(1)} %concatenate.27), channel_id=1, replica_groups=mesh['groups'=2,'blk_0'=32,'blk_1'=2,'head'=4] {'blk_0','blk_1'}, dimensions={2} | all-to-all | bytes 2129920 | tf_op jit(solution)/shard_map/all_to_all | solution.py:24
  241.9 0.1 slice_reduce_fusion.4
  242.0 0.1 fusion.47
  242.1 0.1 div.19
  242.2 1.3 mul.43
  243.6 1.8 mul.44
  245.3 0.6 fusion
  245.9 52.8 %all_gather.13 = bf16[32,2,1,2048]{3,1,2,0:T(2,128)(2,1)S(1)} all-gather(bf16[1,2,1,2048]{3,1,2,0:T(2,128)(2,1)S(1)} %fusion.48), channel_id=1, replica_groups=mesh['groups'=2,'blk_0'=32,'blk_1'=2,'head'=4] {'blk_0'}, dimensions={0}, use_global_device_ids=true | all-gather | bytes 270336 | tf_op jit(solution)/shard_map/all_gather | solution.py:40
  298.7 0.1 copy.28
  298.8 2.2 all-gather
  301.0 0.5 copy.29
  301.6 0.2 copy.30
  301.7 0.3 convolution_bitcast_fusion
  302.1 10.0 %all_to_all.24 = f32[4,2,16,128]{3,2,1,0:T(8,128)S(1)} all-to-all(f32[4,2,16,128]{3,2,1,0:T(8,128)S(1)} %copy.31), channel_id=1, replica_groups=mesh['groups'=2,'blk_0'=32,'blk_1'=2,'head'=4] {'head'}, dimensions={0} | all-to-all | bytes 131072 | tf_op jit(solution)/shard_map/all_to_all | solution.py:58
  312.1 0.6 reduce_sum.72
  (27 shorter events, 0.2 us)
Async XLA Ops:
  0.0 301.7 %copy-start = (bf16[2048,128]{1,0:T(8,128)(2,1)S(1)}, bf16[2048,128]{1,0:T(8,128)(2,1)}, u32[]{:S(2)}) copy-start(bf16[2048,128]{1,0:T(8,128)(2,1)} %param.8) | copy-start | bytes 1572868
  108.6 1.5 copy-start.1
  108.6 1.5 copy-start.2
  114.1 1.3 copy-start.5
  115.6 0.8 copy-start.6
  115.6 0.8 copy-start.4
  115.6 0.9 copy-start.3
where the time goes:
time: 313 us
  blocking collectives  284 us (91%)
  matrix products  13 us (4%)
  local copies, waits for them, and re-layouts  11 us (4%)
  other arithmetic  4.7 us (2%)
    all_to_all x1, blocking collectives, in_one_piece(): lax.all_to_all(both, axis, split_axis=split_dim, concat_axis=concat_dim,...  121 us
    all_gather x1, blocking collectives, body(): piece = lax.all_gather(queries, BLK, axis=1, tiled=True)  97.1 us
    all_gather x2, blocking collectives, gather_in_order(): pieces = lax.all_gather(pieces, axes[k])  55 us
    all_to_all x1, blocking collectives, sent_and_summed(): lax.all_to_all(pieces, axis, split_axis=0, concat_axis=0, tiled=True)  10 us
    dot_general x4, matrix products, body(): jnp.einsum('ngd,cd->ngc', block_query, local_keys, preferred_element_type...  7.44 us

commit v1 on v0

--- a/solution.py
+++ b/solution.py
@@ -67,7 +67,9 @@
     new_count = queries.shape[1] * lax.axis_size(BLK)
     key_pos = lax.axis_index(BLK) * span + jnp.arange(span, dtype=jnp.int32)
     score_scale = 1.0 / math.sqrt(HEAD_DIMENSION)
-    piece = lax.all_gather(queries, BLK, axis=1, tiled=True)
+    piece = jnp.concatenate(
+        lax.all_to_all(jnp.stack([queries] * lax.axis_size(BLK)), BLK, 0, 0), axis=1
+    )
     rows_count = piece.shape[1]
     query_pos = lengths[:, None] - new_count + jnp.arange(rows_count, dtype=jnp.int32)[None, :]
     sums_list = []

time: 313 us -> 328 us (1.048)
  blocking collectives: 284 us -> 186 us
  waiting for transfers between devices: 0 us -> 64 us
  starting transfers between devices: 0 us -> 47.3 us
    all_gather x1 -> x0, blocking collectives: 97.1 us -> none  [body(): piece = lax.all_gather(queries, BLK, axis=1, tiled=True)]
    all_to_all x0 -> x1, waiting for transfers between devices: none -> 64 us  [body(): lax.all_to_all(jnp.stack([queries] * lax.axis_size(BLK)), BLK, 0, 0)]
    all_to_all x0 -> x1, starting transfers between devices: none -> 47.3 us  [body(): lax.all_to_all(jnp.stack([queries] * lax.axis_size(BLK)), BLK, 0, 0)]
  transfers between devices with their start and end apart: 0 -> 1, of which waited for: 0 -> 1; matrix products, arithmetic and copies ran while one was open for 0% -> 0% of each run, Pallas kernels for 0% -> 0%
where the time goes in v1:
time: 328 us
  blocking collectives  186 us (57%)
  waiting for transfers between devices  64 us (20%)
  starting transfers between devices  47.3 us (14%)
  matrix products  13 us (4%)
  local copies, waits for them, and re-layouts  12.9 us (4%)
  other arithmetic  3.99 us (1%)
    all_to_all x1, blocking collectives, in_one_piece(): lax.all_to_all(both, axis, split_axis=split_dim, concat_axis=concat_dim,...  121 us
    all_to_all x1, waiting for transfers between devices, body(): lax.all_to_all(jnp.stack([queries] * lax.axis_size(BLK)), BLK, 0, 0)  64 us
    all_gather x2, blocking collectives, gather_in_order(): pieces = lax.all_gather(pieces, axes[k])  55.5 us
    all_to_all x1, starting transfers between devices, body(): lax.all_to_all(jnp.stack([queries] * lax.axis_size(BLK)), BLK, 0, 0)  47.3 us
    all_to_all x1, blocking collectives, sent_and_summed(): lax.all_to_all(pieces, axis, split_axis=0, concat_axis=0, tiled=True)  10 us
    dot_general x4, matrix products, body(): jnp.einsum('ngd,cd->ngc', block_query, local_keys, preferred_element_type...  7.43 us
  transfers between devices with their start and end apart: 1, of which 1 were waited for; matrix products, arithmetic and copies ran while one was open for 0% of the time, Pallas kernels for 0%

profile of v1, /device:TPU:40, one launch (start us, length us, event | category | flops | bytes accessed | tf_op | source)
XLA Modules:
  0.0 327.7 jit_solution(6491753173265659519)
XLA Ops:
  0.0 1.8 stack.20
  1.8 47.3 %all-to-all-start = ((bf16[64,2,1,2048]{3,1,2,0:T(2,128)(2,1)}), bf16[64,2,1,2048]{3,1,2,0:T(2,128)(2,1)S(1)}, u32[]{:S(2)}, u32[]{:S(2)}) async-start(bf16[64,2,1,2048]{3,1,2,0:T(2,128)(2,1)} %stack.20), calls=%async_computation | async-start | bytes 1048576 | tf_op jit(solution)/shard_map/all_to_all | solution.py:71
  49.2 0.1 iota_add_fusion.1
  49.3 0.1 broadcast_compare_fusion.1
  49.4 64.0 %all-to-all-done = bf16[64,2,1,2048]{3,1,2,0:T(2,128)(2,1)S(1)} async-done(((bf16[64,2,1,2048]{3,1,2,0:T(2,128)(2,1)}), bf16[64,2,1,2048]{3,1,2,0:T(2,128)(2,1)S(1)}, u32[]{:S(2)}, u32[]{:S(2)}) %all-to-all-start) | async-done | bytes 524320 | tf_op jit(solution)/shard_map/all_to_all | solution.py:71
  113.4 2.3 slice_reduce_fusion.3
  115.7 0.7 copy.45
  116.4 1.3 select_reduce_fusion.1
  117.7 0.1 copy.30
  117.8 1.3 fusion.11
  119.1 2.1 fusion.5
  121.2 0.1 copy.31
  121.3 1.3 fusion.9
  122.6 1.3 select_reduce_fusion.3
  123.9 0.1 copy.28
  124.0 1.4 fusion.15
  125.5 2.6 fusion.1
  128.1 0.1 copy.29
  128.1 1.3 fusion.3
  129.5 1.3 fusion.13
  130.8 0.1 copy.35
  130.8 0.1 copy_bitcast_fusion
  131.0 0.4 stack.22
  131.4 0.3 copy-done.6
  131.7 0.1 copy.33
  131.8 0.1 copy.34
  131.8 0.1 copy.36
  131.9 0.1 copy_bitcast_fusion.2
  132.1 0.4 stack.21
  132.5 0.1 copy.32
  132.6 0.1 copy.37
  132.7 0.9 maximum_bitcast_fusion
  133.6 2.1 concatenate.27
  135.8 120.7 %all_to_all.28 = f32[1,2,64,2080]{3,1,0,2:T(2,128)S(1)} all-to-all(f32[1,2,64,2080]{3,1,0,2:T(2,128)S(1)} %concatenate.27), channel_id=1, replica_groups=mesh['groups'=2,'blk_0'=32,'blk_1'=2,'head'=4] {'blk_0','blk_1'}, dimensions={2} | all-to-all | bytes 2129920 | tf_op jit(solution)/shard_map/all_to_all | solution.py:24
  256.5 0.1 slice_reduce_fusion.4
  256.6 0.1 fusion.47
  256.7 0.1 div.19
  256.8 1.3 mul.43
  258.1 1.8 mul.44
  259.9 0.6 fusion
  260.5 53.3 %all_gather.9 = bf16[32,2,1,2048]{3,1,2,0:T(2,128)(2,1)S(1)} all-gather(bf16[1,2,1,2048]{3,1,2,0:T(2,128)(2,1)S(1)} %fusion.48), channel_id=1, replica_groups=mesh['groups'=2,'blk_0'=32,'blk_1'=2,'head'=4] {'blk_0'}, dimensions={0}, use_global_device_ids=true | all-gather | bytes 270336 | tf_op jit(solution)/shard_map/all_gather | solution.py:40
  313.7 0.1 copy.38
  313.8 2.2 all-gather
  316.1 0.5 copy.39
  316.6 0.2 copy.40
  316.8 0.3 convolution_bitcast_fusion
  317.1 10.0 %all_to_all.29 = f32[4,2,16,128]{3,2,1,0:T(8,128)S(1)} all-to-all(f32[4,2,16,128]{3,2,1,0:T(8,128)S(1)} %copy.41), channel_id=1, replica_groups=mesh['groups'=2,'blk_0'=32,'blk_1'=2,'head'=4] {'head'}, dimensions={0} | all-to-all | bytes 131072 | tf_op jit(solution)/shard_map/all_to_all | solution.py:58
  327.1 0.6 reduce_sum.72
  (31 shorter events, 0.2 us)
Async XLA Ops:
  0.0 316.8 %copy-start = (bf16[2048,128]{1,0:T(8,128)(2,1)S(1)}, bf16[2048,128]{1,0:T(8,128)(2,1)}, u32[]{:S(2)}) copy-start(bf16[2048,128]{1,0:T(8,128)(2,1)} %param.8) | copy-start | bytes 1572868
  0.0 49.2 %copy-start.7 = (s32[2]{0:T(128)S(1)}, s32[2]{0:T(128)}, u32[]{:S(2)}) copy-start(s32[2]{0:T(128)} %param.9) | copy-start | bytes 28
  1.8 111.6 %all-to-all-start = ((bf16[64,2,1,2048]{3,1,2,0:T(2,128)(2,1)}), bf16[64,2,1,2048]{3,1,2,0:T(2,128)(2,1)S(1)}, u32[]{:S(2)}, u32[]{:S(2)}) async-start(bf16[64,2,1,2048]{3,1,2,0:T(2,128)(2,1)} %stack.20), calls=%async_computation | async-start | bytes 1048576 | tf_op jit(solution)/shard_map/all_to_all | solution.py:71
  123.9 1.5 copy-start.1
  123.9 1.5 copy-start.2
  129.5 1.3 copy-start.5
  131.0 0.8 copy-start.6
  131.0 0.8 copy-start.4
  131.0 0.9 copy-start.3
